TPU v7x, 128 devices: a whole 4x4x4 slice. The times are simulated.
128 devices in a mesh: seq: 32 (over y, z, core), head: 4 (over x).
Axes of the slice: x: 4, y: 4, z: 4, core: 2. Of those that a mesh axis runs over, the one named last changes fastest.
Arguments:
- inputs: bfloat16 [8192, 2048], P('seq', 'head'), may hold values from -6 to 6
- w_query: bfloat16 [2048, 2048], P(None, 'head'), may hold values from -0.125 to 0.125
- w_key: bfloat16 [2048, 2048], P(None, 'head'), may hold values from -0.125 to 0.125
- w_value: bfloat16 [2048, 2048], P(None, 'head'), may hold values from -0.125 to 0.125
- sketch: float32 [2, 64, 32], replicated, may hold values from -0.75 to 0.75
- prefix_state: float32 [32, 1024, 64], P('head'), may hold values from -112 to 112
- prefix_norm: float32 [32, 1024], P('head'), as said below
- d_attn: bfloat16 [8192, 2048], P('seq', 'head'), may hold values from -256 to 256
- d_state_end: float32 [32, 1024, 64], P('head'), may hold values from -6 to 6
- d_norm_end: float32 [32, 1024], P('head'), may hold values from -4 to 4
Outputs:
- d_input: bfloat16 [8192, 2048], P('seq', 'head')
- d_query: bfloat16 [8192, 2048], P('seq', 'head')
- d_key: bfloat16 [8192, 2048], P('seq', 'head')
- d_value: bfloat16 [8192, 2048], P('seq', 'head')
- d_prefix_state: float32 [32, 1024, 64], P('head')
- d_prefix_norm: float32 [32, 1024], P('head')
Inputs may be any that keep to these rules, and one draw needn't show every extreme that they name: For every head, prefix_norm laid out as a 32 x 32 matrix is symmetric positive semidefinite.
All inputs are finite; a program needn't handle non-finite values.
Results may differ from a plain program's by a relative error of at most 0.012.
Values may be sent and summed in bfloat16 or wider, within the bound.
A program may use at most 192 MiB of HBM per device.

v0:
```python
from functools import partial
import jax
import jax.numpy as jnp
from jax import lax
from jax.sharding import Mesh
from jax.sharding import PartitionSpec as P

SEQ = ("seq_0", "seq_1", "seq_2")
HIGHEST_PRECISION = lax.Precision.HIGHEST


def laid_out(parts, dim):
    lengths = list(parts.shape[1:])
    lengths[dim] *= parts.shape[0]
    return jnp.moveaxis(parts, 0, dim).reshape(lengths)


def copy_for_each(value, axis):
    count = lax.axis_size(axis)
    return lax.all_to_all(
        jnp.broadcast_to(value[None], (count, *value.shape)), axis, 0, 0, tiled=True
    )


def gathered_copies(value, axis, dim):
    return laid_out(copy_for_each(value, axis), dim)


def neutral_like(value, identity):
    return jax.tree.map(
        lambda a, e: jnp.broadcast_to(jnp.asarray(e, a.dtype), a.shape), value, identity
    )


def prefix_by_axis(value, axes, combine, identity):
    before = start = neutral_like(value, identity)
    subtotal = value
    for axis in reversed(axes):
        count, index = (lax.axis_size(axis), lax.axis_index(axis))
        pieces = jax.tree.map(
            lambda part, kind: lax.all_gather(part.astype(kind), axis),
            subtotal,
            (jnp.bfloat16, jnp.bfloat16),
        )
        inside, subtotal = (start, start)
        for k in range(count):
            passed = k < index
            subtotal = combine(
                subtotal, jax.tree.map(lambda part, own: part[k].astype(own.dtype), pieces, value)
            )
            inside = jax.tree.map(lambda new, old: jnp.where(passed, new, old), subtotal, inside)
        before = combine(inside, before)
    return before


def carried_in(value, axes, combine, identity):
    before = start = neutral_like(value, identity)
    subtotal = value
    for axis in reversed(axes):
        count, index = (lax.axis_size(axis), lax.axis_index(axis))
        pieces = jax.tree.map(
            lambda part, kind: lax.all_gather(part.astype(kind), axis),
            subtotal,
            jax.tree.map(lambda a: jnp.bfloat16 if a.dtype == jnp.float32 else a.dtype, value),
        )
        inside, subtotal = (start, start)
        for k in reversed(range(count)):
            passed = k > index
            subtotal = combine(
                subtotal, jax.tree.map(lambda part, own: part[k].astype(own.dtype), pieces, value)
            )
            inside = jax.tree.map(lambda new, old: jnp.where(passed, new, old), subtotal, inside)
        before = combine(inside, before)
    return before


def in_blocks(value, dim, count):
    before, after = (value.shape[:dim], value.shape[dim + 1 :])
    return jnp.moveaxis(value.reshape(*before, count, -1, *after), dim, 0)


def sum_at_owner(value, axis, dim):
    count = lax.axis_size(axis)
    parts = lax.all_to_all(in_blocks(value, dim, count), axis, 0, 0, tiled=True)
    return jnp.sum(parts.astype(jnp.float32), axis=0)


def packed_total(arrays, axis):
    ends = [0]
    for a in arrays:
        ends.append(ends[-1] + a.size)
    subtotal = lax.psum(jnp.concatenate([a.ravel() for a in arrays]), axis)
    return tuple((subtotal[b:e].reshape(a.shape) for a, b, e in zip(arrays, ends, ends[1:])))


def sketch_map(values, sketch):
    left_map = jnp.einsum("hbd,de->hbe", values, sketch[0], precision=HIGHEST_PRECISION)
    right_map = jnp.einsum("hbd,de->hbe", values, sketch[1], precision=HIGHEST_PRECISION)
    return left_map * right_map * sketch.shape[2] ** (-0.5)


def square_features(sketched):
    outer_prod = sketched[:, :, :, None] * sketched[:, :, None, :]
    return outer_prod.reshape(sketched.shape[0], sketched.shape[1], -1)


def attend_block(carried, block_data, sketch):
    value_state, norm_state = carried
    query_block, key_block, value_block = block_data
    sketch_query = sketch_map(query_block, sketch)
    sketch_key = sketch_map(key_block, sketch)
    feat_query = square_features(sketch_query)
    block_size = query_block.shape[1]
    causal = lax.broadcasted_iota(jnp.int32, (block_size, block_size), 0) >= lax.broadcasted_iota(
        jnp.int32, (block_size, block_size), 1
    )
    dot_prod = jnp.einsum("hid,hjd->hij", sketch_query, sketch_key, precision=HIGHEST_PRECISION)
    scores = jnp.where(causal, dot_prod * dot_prod, jnp.zeros_like(dot_prod))
    numerator = jnp.einsum("hif,hfd->hid", feat_query, value_state, precision=HIGHEST_PRECISION)
    numerator = numerator + jnp.einsum(
        "hij,hjd->hid", scores, value_block, precision=HIGHEST_PRECISION
    )
    denominator = (
        1.0
        + jnp.einsum("hif,hf->hi", feat_query, norm_state, precision=HIGHEST_PRECISION)
        + scores.sum(-1)
    )
    outputs = numerator / denominator[:, :, None]
    feat_key = square_features(sketch_key)
    value_state = value_state + jnp.einsum(
        "hjf,hjd->hfd", feat_key, value_block, precision=HIGHEST_PRECISION
    )
    norm_state = norm_state + feat_key.sum(1)
    return ((value_state, norm_state), outputs)


def split_blocks(values, block_size):
    head_count, total_rows, depth_size = values.shape
    return values.reshape(head_count, total_rows // block_size, block_size, depth_size).transpose(
        1, 0, 2, 3
    )


def join_blocks(values):
    block_count, head_count, block_size, depth_size = values.shape
    return values.transpose(1, 0, 2, 3).reshape(head_count, block_count * block_size, depth_size)


def attend_local(query, key, value, value_state, norm_state, sketch):
    block_size = min(query.shape[1], 512)
    block_step = partial(attend_block, sketch=sketch)
    carried, outputs = lax.scan(
        block_step,
        (value_state, norm_state),
        (
            split_blocks(query, block_size),
            split_blocks(key, block_size),
            split_blocks(value, block_size),
        ),
    )
    return join_blocks(outputs)


def local_totals(key, value, sketch):
    block_size = min(key.shape[1], 512)

    def add_block(carried, block_data):
        key_block, value_block = block_data
        feat_key = square_features(sketch_map(key_block, sketch))
        state_sum = carried[0] + jnp.einsum(
            "hjf,hjd->hfd", feat_key, value_block, precision=HIGHEST_PRECISION
        )
        return ((state_sum, carried[1] + feat_key.sum(1)), None)

    feat_size = sketch.shape[2] * sketch.shape[2]
    start_state = jnp.zeros((key.shape[0], feat_size, key.shape[2]), jnp.float32)
    start_norm = jnp.zeros((key.shape[0], feat_size), jnp.float32)
    carried, unused = lax.scan(
        add_block,
        (start_state, start_norm),
        (split_blocks(key, block_size), split_blocks(value, block_size)),
    )
    return carried


def add_pair(earlier, later):
    return (earlier[0] + later[0], earlier[1] + later[1])


def pull_weight(gradient, weight):
    return lax.dot_general(
        gradient, weight, (((1,), (1,)), ((), ())), preferred_element_type=jnp.float32
    )


def body(
    inputs,
    w_query,
    w_key,
    w_value,
    sketch,
    prefix_state,
    prefix_norm,
    d_attn,
    d_state_end,
    d_norm_end,
):
    tok_rows = inputs.shape[0]
    width = w_query.shape[1]
    head_count = prefix_state.shape[0]
    head_size = width // head_count
    shard_cols = gathered_copies(inputs, "head", 1)
    query, key, value = tuple(
        (
            jnp.dot(shard_cols, weight, preferred_element_type=jnp.float32)
            for weight in (w_query, w_key, w_value)
        )
    )

    def to_heads(values):
        return (
            values.reshape(tok_rows, head_count, head_size).transpose(1, 0, 2).astype(jnp.float32)
        )

    def flatten(values):
        return values.transpose(1, 0, 2).reshape(tok_rows, width).astype(jnp.bfloat16)

    query_heads = to_heads(lax.optimization_barrier(query.astype(jnp.bfloat16)))
    key_heads = to_heads(lax.optimization_barrier(key.astype(jnp.bfloat16)))
    value_heads = to_heads(lax.optimization_barrier(value.astype(jnp.bfloat16)))

    def totals_of(key_in, value_in):
        return local_totals(key_in, value_in, sketch)

    (state_here, norm_here), pull_totals = jax.vjp(totals_of, key_heads, value_heads)
    zero_state = jnp.zeros_like(prefix_state)
    zero_norm = jnp.zeros_like(prefix_norm)
    state_before, norm_before = prefix_by_axis(
        (state_here, norm_here), SEQ, add_pair, (zero_state, zero_norm)
    )
    state_prev = prefix_state + state_before
    norm_prev = prefix_norm + norm_before

    def outputs_of(query_in, key_in, value_in, state_in, norm_in):
        return attend_local(query_in, key_in, value_in, state_in, norm_in, sketch)

    unused, pull_local = jax.vjp(
        outputs_of, query_heads, key_heads, value_heads, state_prev, norm_prev
    )
    grad_query, grad_key, grad_value, cot_state, cot_norm = pull_local(to_heads(d_attn))
    d_query = flatten(grad_query)
    state_after, norm_after = carried_in(
        (cot_state, cot_norm), SEQ, add_pair, (zero_state, zero_norm)
    )
    state_after = d_state_end + state_after
    norm_after = d_norm_end + norm_after
    extra_key, extra_value = pull_totals((state_after, norm_after))
    d_key = flatten(grad_key + extra_key)
    d_value = flatten(grad_value + extra_value)
    whole_term = (
        pull_weight(d_query, w_query) + pull_weight(d_key, w_key) + pull_weight(d_value, w_value)
    )
    d_input = sum_at_owner(whole_term.astype(jnp.bfloat16), "head", 1).astype(jnp.bfloat16)
    total_state, total_norm = tuple(
        (
            part.astype(jnp.float32)
            for part in packed_total(
                (cot_state.astype(jnp.bfloat16), cot_norm.astype(jnp.bfloat16)), SEQ
            )
        )
    )
    d_prefix_state = d_state_end + total_state
    d_prefix_norm = d_norm_end + total_norm
    return (d_input, d_query, d_key, d_value, d_prefix_state, d_prefix_norm)


def solution(mesh):
    finer = Mesh(
        mesh.devices.reshape(4, 4, 2, mesh.shape["head"]), ("seq_0", "seq_1", "seq_2", "head")
    )
    return jax.shard_map(
        body,
        mesh=finer,
        in_specs=(
            P(SEQ, "head"),
            P(None, "head"),
            P(None, "head"),
            P(None, "head"),
            P(),
            P("head", None, None),
            P("head", None),
            P(SEQ, "head"),
            P("head", None, None),
            P("head", None),
        ),
        out_specs=(
            P(SEQ, "head"),
            P(SEQ, "head"),
            P(SEQ, "head"),
            P(SEQ, "head"),
            P("head", None, None),
            P("head", None),
        ),
        check_vma=False,
    )
```

profile of v0, /device:TPU:1, one launch (start us, length us, event | category | flops | bytes accessed | tf_op | source)
XLA Modules:
  0.0 514.4 jit_solution(4007921592596742459)
XLA Ops:
  9.5 4.8 all-to-all-start
  14.5 14.2 %all-to-all-done = bf16[4,256,512]{1,2,0:T(8,128)(2,1)} async-done(((bf16[4,256,512]{1,2,0:T(8,128)(2,1)}), bf16[4,256,512]{1,2,0:T(8,128)(2,1)}, u32[]{:S(2)}, u32[]{:S(2)}) %all-to-all-start) | async-done | bytes 1048608 | tf_op jit(solution)/shard_map/all_to_all | solution.py:20
  45.3 5.6 %multiply_reduce_fusion.2 = (f32[8,256,32]{1,2,0:T(8,128)}, bf16[8,32,32]{2,1,0:T(8,128)(2,1)}, f32[8,256,32]{1,2,0:T(8,128)}, f32[8,256,32,32]{1,3,2,0:T(8,128)}) fusion(f32[8,256,32]{1,2,0:T(8,128)S(1)} %get-tuple-element.403, f32[8,256,1024]{1,2,0:T(8,128)S(1)} %fusion.49, f32[8,256,32,32]{1,3,2,0:T(8,128)S(1)} %bitcast.171), kind=kLoop, calls=%fused_computation.2 | loop fusion | flops 12443648 | bytes 25968640 | tf_op jit(solution)/shard_map/transpose(jvp())/while/body/eval_jaxpr/reduce_sum | solution.py:103
  55.8 10.4 %all_gather.55 = bf16[4,8,1024]{2,1,0:T(8,128)(2,1)S(1)} all-gather(bf16[1,8,1024]{2,1,0:T(8,128)(2,1)S(1)} %fusion.92), channel_id=1, replica_groups=mesh['seq_0'=4,'seq_1'=4,'seq_2'=2,'head'=4] {'seq_1'}, dimensions={0}, use_global_device_ids=true | all-gather | bytes 81920 | tf_op jit(solution)/shard_map/all_gather | solution.py:41
  66.9 10.4 %all_gather.56 = bf16[4,8,1024]{2,1,0:T(8,128)(2,1)} all-gather(bf16[1,8,1024]{2,1,0:T(8,128)(2,1)S(1)} %fusion.91), channel_id=1, replica_groups=mesh['seq_0'=4,'seq_1'=4,'seq_2'=2,'head'=4] {'seq_0'}, dimensions={0}, use_global_device_ids=true | all-gather | bytes 81920 | tf_op jit(solution)/shard_map/all_gather | solution.py:41
  77.3 8.7 %convolution_convert_fusion.1 = bf16[8,1024,64]{1,2,0:T(8,128)(2,1)} fusion(f32[8,256,1024]{1,2,0:T(8,128)} %bitcast.168, bf16[8,256,64]{1,2,0:T(8,128)(2,1)S(1)} %bitcast.176), kind=kOutput, calls=%fused_computation.64 | convolution fusion | flops 1611137024 | bytes 9699328 | tf_op jit(solution)/shard_map/jvp()/while/body/eval_jaxpr/hjf,hjd->hfd/dot_general | solution.py:170
  91.4 4.4 fusion.87
  95.9 9.6 %convolution_convert_fusion = bf16[8,1024,64]{1,2,0:T(8,128)(2,1)} fusion(f32[8,256,1024]{1,2,0:T(8,128)S(1)} %bitcast.165, f32[8,256]{1,0:T(8,128)S(1)} %get-tuple-element.397, f32[256,512]{0,1:T(8,128)S(1)} %copy.59), kind=kOutput, calls=%fused_computation.63 | convolution fusion | flops 1611268096 | bytes 9969664 | tf_op jit(solution)/shard_map/transpose(jvp())/while/body/eval_jaxpr/hif,hfd->hid/dot_general | solution.py:119
  108.6 14.7 %all-gather.20.cloned.1.call-done = bf16[16,1024,64]{1,2,0:T(8,128)(2,1)} async-done(((bf16[8,1024,64]{1,2,0:T(8,128)(2,1)}), bf16[16,1024,64]{1,2,0:T(8,128)(2,1)}) %all-gather.20.cloned.1.call-update) | async-done | bytes 2097168 | tf_op jit(solution)/shard_map/all_gather | solution.py:62
  126.3 47.9 %all-gather.10.cloned.1.call-done = bf16[4,8,1024,64]{2,3,1,0:T(8,128)(2,1)} async-done(((bf16[1,8,1024,64]{2,3,1,0:T(8,128)(2,1)}), bf16[4,8,1024,64]{2,3,1,0:T(8,128)(2,1)}) %all-gather.10.cloned.1.call-update) | async-done | bytes 4194320 | tf_op jit(solution)/shard_map/all_gather | solution.py:41
  174.2 4.1 fusion.29
  178.3 46.0 %all-gather.14.cloned.1.call-done = bf16[4,8,1024,64]{2,3,1,0:T(8,128)(2,1)} async-done(((bf16[1,8,1024,64]{2,3,1,0:T(8,128)(2,1)}), bf16[4,8,1024,64]{2,3,1,0:T(8,128)(2,1)}) %all-gather.14.cloned.1.call-update) | async-done | bytes 4194320 | tf_op jit(solution)/shard_map/all_gather | solution.py:62
  224.3 4.1 fusion.28
  239.1 8.6 %fusion.47 = f32[8,256,64]{1,2,0:T(8,128)} fusion(f32[8,256,1024]{1,2,0:T(8,128)} %bitcast.169), kind=kOutput, calls=%fused_computation.90 | convolution fusion | flops 1610612736 | bytes 8912896 | tf_op jit(solution)/shard_map/transpose(jvp())/while/body/eval_jaxpr/hjf,hjd->hfd/dot_general | solution.py:130
  247.7 26.6 %all-gather.12.cloned.1.call-done = bf16[4,8,1024,64]{2,3,1,0:T(8,128)(2,1)} async-done(((bf16[1,8,1024,64]{2,3,1,0:T(8,128)(2,1)}), bf16[4,8,1024,64]{2,3,1,0:T(8,128)(2,1)}) %all-gather.12.cloned.1.call-update) | async-done | bytes 4194320 | tf_op jit(solution)/shard_map/all_gather | solution.py:41
  274.3 5.9 %fusion.8 = f32[8,1024,64]{1,2,0:T(8,128)S(1)} fusion(f32[8,1024,64]{1,2,0:T(8,128)} %param.15, bf16[4,8,1024,64]{2,3,1,0:T(8,128)(2,1)} %all-gather.12.cloned.1.call-done, pred[]{:T(512)S(6)} %gt.38, pred[]{:T(512)S(6)} %gt.39, pred[]{:T(512)S(6)} %gt.34, pred[]{:T(512)S(6)} %gt.30, pred[]{:T(512)S(6)} %gt.37, pred[]{:T(512)S(6)} %gt.36, pred[]{:T(512)S(6)} %gt.35, ...), kind=kLoop, calls=%fused_computation.32 | loop fusion | flops 15728640 | bytes 14680074 | tf_op jit(solution)/shard_map/add | solution.py:241
  280.2 8.3 %fusion.128 = f32[8,256,64]{1,2,0:T(8,128)S(1)} fusion(f32[8,256,1024]{1,2,0:T(8,128)} %bitcast.166, f32[8,1024,64]{1,2,0:T(8,128)S(1)} %fusion.8), kind=kOutput, calls=%fused_computation.197 | convolution fusion | flops 1610612736 | bytes 11010048 | tf_op jit(solution)/shard_map/jvp()/while/body/eval_jaxpr/hif,hfd->hid/dot_general | solution.py:119
  289.6 10.2 %fusion.119 = bf16[8,1,1024]{2,1,0:T(2,128)(2,1)S(1)} fusion(f32[8,256,1024]{1,2,0:T(8,128)} %bitcast.167, f32[8,256,1]{1,0,2:T(8,128)S(1)} %get-tuple-element.399), kind=kOutput, calls=%fused_computation.187 | convolution fusion | flops 25165824 | bytes 8413184 | tf_op jit(solution)/shard_map/transpose(jvp())/while/body/eval_jaxpr/hif,hf->hi/dot_general | solution.py:125
  301.0 9.3 %multiply_add_fusion = f32[8,256,1024]{2,1,0:T(8,128)} fusion(f32[8,1024]{1,0:T(8,128)S(1)} %fusion.68, f32[8,256]{1,0:T(8,128)S(1)} %get-tuple-element.400, f32[8,1024,64]{1,2,0:T(8,128)S(1)} %fusion.8, f32[8,256]{1,0:T(8,128)S(1)} %get-tuple-element.397, f32[256,512]{0,1:T(8,128)S(1)} %copy.59), kind=kOutput, calls=%fused_computation.6 | convolution fusion | flops 1614938112 | bytes 11059200 | tf_op jit(solution)/shard_map/transpose(jvp())/while/body/eval_jaxpr/hif,hfd->hid/dot_general | solution.py:119
  310.3 9.2 %copy.66 = f32[8,256,1024]{1,2,0:T(8,128)} copy(f32[8,256,1024]{2,1,0:T(8,128)} %multiply_add_fusion) | data formatting | bytes 16777216 | tf_op jit(solution)/shard_map/transpose(jvp())/while/body/eval_jaxpr/hif,hfd->hid/add_any | solution.py:119
  322.3 8.9 %multiply_reduce_fusion.5 = (f32[8,256,32]{1,2,0:T(8,128)S(1)}, f32[8,256,32]{1,2,0:T(8,128)S(1)}) fusion(f32[8,256,32,32]{1,3,2,0:T(8,128)} %bitcast.172, f32[8,256,32]{1,2,0:T(8,128)S(1)} %get-tuple-element.401, f32[8,256,1024]{1,2,0:T(8,128)} %copy.66), kind=kLoop, calls=%fused_computation.5 | loop fusion | flops 8257536 | bytes 17563648 | tf_op jit(solution)/shard_map/transpose(jvp())/while/body/eval_jaxpr/reduce_sum | solution.py:103
  338.9 9.4 %all_gather.63 = bf16[4,8,1024]{2,1,0:T(8,128)(2,1)S(1)} all-gather(bf16[1,8,1024]{2,1,0:T(8,128)(2,1)S(1)} %fusion.93), channel_id=1, replica_groups=mesh['seq_0'=4,'seq_1'=4,'seq_2'=2,'head'=4] {'seq_1'}, dimensions={0}, use_global_device_ids=true | all-gather | bytes 81920 | tf_op jit(solution)/shard_map/all_gather | solution.py:62
  349.0 9.7 %all_gather.64 = bf16[4,8,1024]{2,1,0:T(8,128)(2,1)} all-gather(bf16[1,8,1024]{2,1,0:T(8,128)(2,1)S(1)} %fusion.90), channel_id=1, replica_groups=mesh['seq_0'=4,'seq_1'=4,'seq_2'=2,'head'=4] {'seq_0'}, dimensions={0}, use_global_device_ids=true | all-gather | bytes 81920 | tf_op jit(solution)/shard_map/all_gather | solution.py:62
  361.8 5.9 %fusion.18 = f32[8,1024,64]{1,2,0:T(8,128)S(1)} fusion(f32[8,1024,64]{1,2,0:T(8,128)} %param.18, bf16[4,8,1024,64]{2,3,1,0:T(8,128)(2,1)} %all-gather.16.cloned.1.call-done, pred[]{:T(512)S(6)} %lt.44, pred[]{:T(512)S(6)} %lt.45, pred[]{:T(512)S(6)} %lt.40, pred[]{:T(512)S(6)} %lt.36, pred[]{:T(512)S(6)} %lt.43, pred[]{:T(512)S(6)} %lt.42, pred[]{:T(512)S(6)} %lt.41, ...), kind=kLoop, calls=%fused_computation.42 | loop fusion | flops 15728640 | bytes 14680074 | tf_op jit(solution)/shard_map/add | solution.py:255
  367.7 9.5 %fusion.130 = f32[8,256,64]{1,2,0:T(8,128)} fusion(f32[8,256,1024]{1,2,0:T(8,128)} %bitcast.170, f32[8,1024,64]{1,2,0:T(8,128)S(1)} %fusion.18), kind=kOutput, calls=%fused_computation.199 | convolution fusion | flops 1610612736 | bytes 11010048 | tf_op jit(solution)/shard_map/transpose(jvp())/while/body/eval_jaxpr/hjf,hjd->hfd/dot_general | solution.py:170
  379.2 7.5 %broadcast_add_fusion = f32[8,256,1024]{2,1,0:T(8,128)} fusion(f32[8,1024]{1,0:T(8,128)S(1)} %fusion.81, bf16[8,256,64]{1,2,0:T(8,128)(2,1)S(1)} %bitcast.179, f32[8,1024,64]{1,2,0:T(8,128)} %copy-done.6), kind=kOutput, calls=%fused_computation.7 | convolution fusion | flops 1612709888 | bytes 10780672 | tf_op jit(solution)/shard_map/transpose(jvp())/while/body/eval_jaxpr/hjf,hjd->hfd/dot_general | solution.py:170
  386.8 9.1 %copy.70 = f32[8,256,1024]{1,2,0:T(8,128)} copy(f32[8,256,1024]{2,1,0:T(8,128)} %broadcast_add_fusion) | data formatting | bytes 16777216 | tf_op jit(solution)/shard_map/transpose(jvp())/while/body/eval_jaxpr/hjf,hjd->hfd/add_any | solution.py:170
  395.9 9.0 %multiply_reduce_fusion = (f32[8,256,32]{1,2,0:T(8,128)S(1)}, f32[8,256,32]{1,2,0:T(8,128)S(1)}) fusion(f32[8,256,32]{1,2,0:T(8,128)S(1)} %get-tuple-element.403, f32[8,256,1024]{1,2,0:T(8,128)} %copy.70, f32[8,256,32,32]{1,3,2,0:T(8,128)} %bitcast.173), kind=kLoop, calls=%fused_computation | loop fusion | flops 8257536 | bytes 17563648 | tf_op jit(solution)/shard_map/transpose(jvp())/while/body/eval_jaxpr/reduce_sum | solution.py:103
  410.4 4.5 convolution_add_fusion.1
  426.1 62.0 %all-reduce.2.cloned.1.call-done = bf16[532480]{0:T(1024)(128)(2,1)} async-done(((bf16[532480]{0:T(1024)(128)(2,1)}), bf16[532480]{0:T(1024)(128)(2,1)}) %all-reduce.2.cloned.1.call-update) | async-done | bytes 1064976 | tf_op jit(solution)/shard_map/psum | solution.py:92
  492.2 4.3 reshape.415
  496.5 5.9 %add.295 = f32[8,1024,64]{2,1,0:T(8,128)} add(f32[8,1024,64]{2,1,0:T(8,128)} %copy.76, f32[8,1024,64]{2,1,0:T(8,128)} %reshape.415) | non-fusion elementwise | flops 524288 | bytes 6291456 | tf_op jit(solution)/shard_map/add | solution.py:272
  (130 shorter events, 90.6 us)
Async XLA Ops:
  7.2 27.6 %copy-start = (bf16[2048,512]{1,0:T(8,128)(2,1)S(1)}, bf16[2048,512]{1,0:T(8,128)(2,1)}, u32[]{:S(2)}) copy-start(bf16[2048,512]{1,0:T(8,128)(2,1)} %param.11) | copy-start | bytes 6291460
  7.2 7.1 %copy-start.23 = (bf16[256,512]{1,0:T(8,128)(2,1)S(1)}, bf16[256,512]{1,0:T(8,128)(2,1)}, u32[]{:S(2)}) copy-start(bf16[256,512]{1,0:T(8,128)(2,1)} %param.17) | copy-start | bytes 786436
  9.5 19.2 %all-to-all-start = ((bf16[4,256,512]{1,2,0:T(8,128)(2,1)}), bf16[4,256,512]{1,2,0:T(8,128)(2,1)}, u32[]{:S(2)}, u32[]{:S(2)}) async-start(bf16[4,256,512]{1,2,0:T(8,128)(2,1)} %broadcast_in_dim.136), calls=%async_computation | async-start | bytes 2097152 | tf_op jit(solution)/shard_map/all_to_all | solution.py:20
  14.3 91.2 %all-gather.18.cloned.1.call-start = ((), (), s32[]{:S(2)}) async-start(), calls=%async_computation.7 | async-start | bytes 3145728 | tf_op jit(solution)/shard_map/all_gather | solution.py:41
  34.8 3.2 copy-start.17
  38.0 0.7 copy-start.10
  38.3 3.6 copy-start.8
  39.0 2.9 copy-start.11
  86.0 37.3 %all-gather.20.cloned.1.call-start = ((), (), s32[]{:S(2)}) async-start(), calls=%async_computation.8 | async-start | bytes 3145728 | tf_op jit(solution)/shard_map/all_gather | solution.py:62
  91.4 4.4 copy-start.1
  105.4 68.7 %all-gather.10.cloned.1.call-start = ((), (), s32[]{:S(2)}) async-start(), calls=%async_computation.2 | async-start | bytes 5242880 | tf_op jit(solution)/shard_map/all_gather | solution.py:41
  108.5 115.8 %all-gather.14.cloned.1.call-start = ((), (), s32[]{:S(2)}) async-start(), calls=%async_computation.4 | async-start | bytes 5242880 | tf_op jit(solution)/shard_map/all_gather | solution.py:62
  126.3 148.0 %all-gather.12.cloned.1.call-start = ((), (), s32[]{:S(2)}) async-start(), calls=%async_computation.3 | async-start | bytes 5242880 | tf_op jit(solution)/shard_map/all_gather | solution.py:41
  178.3 183.5 %all-gather.16.cloned.1.call-start = ((), (), s32[]{:S(2)}) async-start(), calls=%async_computation.5 | async-start | bytes 5242880 | tf_op jit(solution)/shard_map/all_gather | solution.py:62
  228.4 259.7 %all-reduce.2.cloned.1.call-start = ((), (), s32[]{:S(2)}) async-start(), calls=%async_computation.6 | async-start | bytes 2129920 | tf_op jit(solution)/shard_map/psum | solution.py:92
  280.1 8.3 %copy-start.2 = (f32[8,256,256]{1,2,0:T(8,128)S(1)}, f32[8,256,256]{1,2,0:T(8,128)}, u32[]{:S(2)}) copy-start(f32[8,256,256]{1,2,0:T(8,128)} %get-tuple-element.406) | copy-start | bytes 6291460
  322.3 9.0 %copy-start.4 = (f32[8,256,256]{1,2,0:T(8,128)}, f32[8,256,256]{1,2,0:T(8,128)S(1)}, u32[]{:S(2)}) copy-start(f32[8,256,256]{1,2,0:T(8,128)S(1)} %add_multiply_fusion) | copy-start | bytes 6291460
  331.2 1.4 copy-start.16
  331.3 2.0 copy-start.12
  367.6 9.5 %copy-start.6 = (f32[8,1024,64]{1,2,0:T(8,128)}, f32[8,1024,64]{1,2,0:T(8,128)S(1)}, u32[]{:S(2)}) copy-start(f32[8,1024,64]{1,2,0:T(8,128)S(1)} %fusion.18) | copy-start | bytes 6291460
  367.6 9.5 %copy-start.7 = (bf16[524288]{0:T(1024)(128)(2,1)S(1)}, bf16[524288]{0:T(1024)(128)(2,1)}, u32[]{:S(2)}) copy-start(bf16[524288]{0:T(1024)(128)(2,1)} %reshape.397) | copy-start | bytes 3145732
  367.7 9.5 %copy-start.25 = (bf16[1,8,8,128]{3,1,2,0:T(8,128)(2,1)S(1)}, bf16[1,8,8,128]{3,1,2,0:T(8,128)(2,1)}, u32[]{:S(2)}) copy-start(bf16[1,8,8,128]{3,1,2,0:T(8,128)(2,1)} %copy.111) | copy-start | bytes 49156
  395.9 9.0 %copy-start.5 = (f32[8,256,256]{1,2,0:T(8,128)S(1)}, f32[8,256,256]{1,2,0:T(8,128)}, u32[]{:S(2)}) copy-start(f32[8,256,256]{1,2,0:T(8,128)} %copy-done.4) | copy-start | bytes 6291460
  395.9 9.0 %copy-start.14 = (f32[8,256,32]{1,2,0:T(8,128)S(1)}, f32[8,256,32]{1,2,0:T(8,128)}, u32[]{:S(2)}) copy-start(f32[8,256,32]{1,2,0:T(8,128)} %get-tuple-element.389) | copy-start | bytes 786436
  395.9 9.0 %copy-start.15 = (f32[8,256,32]{1,2,0:T(8,128)S(1)}, f32[8,256,32]{1,2,0:T(8,128)}, u32[]{:S(2)}) copy-start(f32[8,256,32]{1,2,0:T(8,128)} %get-tuple-element.391) | copy-start | bytes 786436
  404.9 2.1 copy-start.13
  404.9 3.3 copy-start.9
  410.4 4.5 copy-start.3
  410.4 4.5 copy-start.20
  410.4 4.5 copy-start.21
  422.2 84.0 %all-to-all-start.1 = ((bf16[4,256,512]{2,1,0:T(8,128)(2,1)}), bf16[4,256,512]{2,1,0:T(8,128)(2,1)S(1)}, u32[]{:S(2)}, u32[]{:S(2)}) async-start(bf16[4,256,512]{2,1,0:T(8,128)(2,1)} %bitcast.180), calls=%async_computation.1 | async-start | bytes 2097152 | tf_op jit(solution)/shard_map/all_to_all | solution.py:84
  426.1 65.4 %copy-start.24 = (f32[8,1024]{1,0:T(8,128)S(1)}, f32[8,1024]{1,0:T(8,128)}, u32[]{:S(2)}) copy-start(f32[8,1024]{1,0:T(8,128)} %param.19) | copy-start | bytes 98308
  (3 other events, 1.9 us)
Sparse Core Ops, SparseCore 0:
  86.1 17.6 all-gather.17
  105.6 17.6 all-gather.19
  125.0 49.1 all-gather.9
  175.7 48.5 all-gather.13
  225.8 48.3 all-gather.11
  275.8 48.5 all-gather.15
  378.4 109.6 all-reduce.1
where the time goes:
time: 522 us; the launch traced here: 514 us
  waiting for transfers between devices  211 us (40%)
  matrix products  119 us (23%)
  other arithmetic  64.3 us (12%)
  local copies, waits for them, and re-layouts  49.9 us (10%)
  blocking collectives  45.8 us (9%)
  between operations  15.1 us (3%)
  starting transfers between devices  9.05 us (2%)
    all_gather x3, waiting for transfers between devices, prefix_by_axis(): lax.all_gather(part.astype(kind), axis)  74.4 us
    psum x1, waiting for transfers between devices, packed_total(): subtotal = lax.psum(jnp.concatenate([a.ravel() for a in arrays]), axis)  62 us
    all_gather x3, waiting for transfers between devices, carried_in(): lax.all_gather(part.astype(kind), axis)  60.7 us
    dot_general x3, matrix products, attend_block(): jnp.einsum('hif,hfd->hid', feat_query, value_state, precision=HIGHEST_PRE...  27.1 us
    dot_general x3, matrix products, add_block(): jnp.einsum('hjf,hjd->hfd', feat_key, value_block, precision=HIGHEST_PRECI...  25.8 us
    all_gather x3, blocking collectives, prefix_by_axis(): lax.all_gather(part.astype(kind), axis)  24.1 us
    reduce_sum x3, other arithmetic, square_features(): outer_prod = sketched[:, :, :, None] * sketched[:, :, None, :]  23.6 us
    all_gather x3, blocking collectives, carried_in(): lax.all_gather(part.astype(kind), axis)  21.7 us
  transfers between devices with their start and end apart: 9, of which 6 were waited for; matrix products, arithmetic and copies ran while one was open for 35% of the time, Pallas kernels for 0%

commit v1 on v0

--- a/solution.py
+++ b/solution.py
@@ -89,7 +89,7 @@
     ends = [0]
     for a in arrays:
         ends.append(ends[-1] + a.size)
-    subtotal = lax.psum(jnp.concatenate([a.ravel() for a in arrays]), axis)
+    subtotal = jnp.sum(lax.all_gather(jnp.concatenate([a.ravel() for a in arrays]), axis), axis=0)
     return tuple((subtotal[b:e].reshape(a.shape) for a, b, e in zip(arrays, ends, ends[1:])))
 
 

time: 522 us -> 538 us (1.031)
  local copies, waits for them, and re-layouts: 49.9 us -> 96.2 us
  waiting for transfers between devices: 211 us -> 179 us
  other arithmetic: 64.3 us -> 79.7 us
  matrix products: 119 us -> 104 us
    psum x1 -> x0, waiting for transfers between devices: 62 us -> none  [packed_total(): subtotal = lax.psum(jnp.concatenate([a.ravel() for a in arrays]), axis)]
    all_gather x0 -> x1, local copies, waits for them, and re-layouts: none -> 41.3 us  [packed_total(): lax.all_gather(jnp.concatenate([a.ravel() for a in arrays]), axis)]
    reduce_sum x0 -> x1, other arithmetic: none -> 22.7 us  [packed_total(): jnp.sum(lax.all_gather(jnp.concatenate([a.ravel() for a in arrays]), axis...]
    all_gather x3, waiting for transfers between devices: 74.4 us -> 93.7 us  [prefix_by_axis(): lax.all_gather(part.astype(kind), axis)]
    all_gather x0 -> x1, waiting for transfers between devices: none -> 15.5 us  [packed_total(): lax.all_gather(jnp.concatenate([a.ravel() for a in arrays]), axis)]
    dot_general x3, matrix products: 10.5 us -> 2.3 us  [pull_weight(): lax.dot_general(gradient, weight, (((1,), (1,)), ((), ())), preferred_ele...]
    all_gather x3, waiting for transfers between devices: 60.7 us -> 54.1 us  [carried_in(): lax.all_gather(part.astype(kind), axis)]
    dot_general x3, matrix products: 25.8 us -> 20.1 us  [add_block(): jnp.einsum('hjf,hjd->hfd', feat_key, value_block, precision=HIGHEST_PRECI...]
  transfers between devices with their start and end apart: 9 -> 9, of which waited for: 6 -> 7; matrix products, arithmetic and copies ran while one was open for 35% -> 30% of each run, Pallas kernels for 0% -> 0%
where the time goes in v1:
time: 538 us; the launch traced here: 530 us
  waiting for transfers between devices  179 us (33%)
  matrix products  104 us (19%)
  local copies, waits for them, and re-layouts  96.2 us (18%)
  other arithmetic  79.7 us (15%)
  blocking collectives  46.7 us (9%)
  between operations  15 us (3%)
  starting transfers between devices  9.09 us (2%)
    all_gather x3, waiting for transfers between devices, prefix_by_axis(): lax.all_gather(part.astype(kind), axis)  93.7 us
    all_gather x3, waiting for transfers between devices, carried_in(): lax.all_gather(part.astype(kind), axis)  54.1 us
    all_gather x1, local copies, waits for them, and re-layouts, packed_total(): lax.all_gather(jnp.concatenate([a.ravel() for a in arrays]), axis)  41.3 us
    dot_general x3, matrix products, attend_block(): jnp.einsum('hif,hfd->hid', feat_query, value_state, precision=HIGHEST_PRE...  27.6 us
    all_gather x3, blocking collectives, prefix_by_axis(): lax.all_gather(part.astype(kind), axis)  24.1 us
    reduce_sum x1, other arithmetic, packed_total(): jnp.sum(lax.all_gather(jnp.concatenate([a.ravel() for a in arrays]), axis...  22.7 us
    all_gather x3, blocking collectives, carried_in(): lax.all_gather(part.astype(kind), axis)  22.6 us
    unnamed x75, local copies, waits for them, and re-layouts  20.2 us
  transfers between devices with their start and end apart: 9, of which 7 were waited for; matrix products, arithmetic and copies ran while one was open for 30% of the time, Pallas kernels for 0%

profile of v1, /device:TPU:1, one launch (start us, length us, event | category | flops | bytes accessed | tf_op | source)
XLA Modules:
  0.0 530.0 jit_solution(13519860056708522363)
XLA Ops:
  9.5 4.8 all-to-all-start
  14.5 14.2 %all-to-all-done = bf16[4,256,512]{1,2,0:T(8,128)(2,1)} async-done(((bf16[4,256,512]{1,2,0:T(8,128)(2,1)}), bf16[4,256,512]{1,2,0:T(8,128)(2,1)}, u32[]{:S(2)}, u32[]{:S(2)}) %all-to-all-start) | async-done | bytes 1048608 | tf_op jit(solution)/shard_map/all_to_all | solution.py:20
  45.2 5.6 %multiply_reduce_fusion.2 = (f32[8,256,32]{1,2,0:T(8,128)}, bf16[8,32,32]{2,1,0:T(8,128)(2,1)}, f32[8,256,32]{1,2,0:T(8,128)}, f32[8,256,32,32]{1,3,2,0:T(8,128)}) fusion(f32[8,256,32]{1,2,0:T(8,128)S(1)} %get-tuple-element.409, f32[8,256,1024]{1,2,0:T(8,128)S(1)} %fusion.49, f32[8,256,32,32]{1,3,2,0:T(8,128)S(1)} %bitcast.173), kind=kLoop, calls=%fused_computation.2 | loop fusion | flops 12443648 | bytes 25968640 | tf_op jit(solution)/shard_map/transpose(jvp())/while/body/eval_jaxpr/reduce_sum | solution.py:103
  55.7 10.4 %all_gather.61 = bf16[4,8,1024]{2,1,0:T(8,128)(2,1)S(1)} all-gather(bf16[1,8,1024]{2,1,0:T(8,128)(2,1)S(1)} %fusion.92), channel_id=1, replica_groups=mesh['seq_0'=4,'seq_1'=4,'seq_2'=2,'head'=4] {'seq_1'}, dimensions={0}, use_global_device_ids=true | all-gather | bytes 81920 | tf_op jit(solution)/shard_map/all_gather | solution.py:41
  66.8 10.4 %all_gather.62 = bf16[4,8,1024]{2,1,0:T(8,128)(2,1)} all-gather(bf16[1,8,1024]{2,1,0:T(8,128)(2,1)S(1)} %fusion.91), channel_id=1, replica_groups=mesh['seq_0'=4,'seq_1'=4,'seq_2'=2,'head'=4] {'seq_0'}, dimensions={0}, use_global_device_ids=true | all-gather | bytes 81920 | tf_op jit(solution)/shard_map/all_gather | solution.py:41
  77.2 8.7 %convolution_convert_fusion.1 = bf16[8,1024,64]{1,2,0:T(8,128)(2,1)} fusion(f32[8,256,1024]{1,2,0:T(8,128)} %bitcast.168, bf16[8,256,64]{1,2,0:T(8,128)(2,1)S(1)} %bitcast.180), kind=kOutput, calls=%fused_computation.64 | convolution fusion | flops 1611137024 | bytes 9699328 | tf_op jit(solution)/shard_map/jvp()/while/body/eval_jaxpr/hjf,hjd->hfd/dot_general | solution.py:170
  91.3 4.4 fusion.87
  95.8 9.6 %convolution_convert_fusion = bf16[8,1024,64]{1,2,0:T(8,128)(2,1)} fusion(f32[8,256,1024]{1,2,0:T(8,128)S(1)} %bitcast.165, f32[8,256]{1,0:T(8,128)S(1)} %get-tuple-element.403, f32[256,512]{0,1:T(8,128)S(1)} %copy.84), kind=kOutput, calls=%fused_computation.63 | convolution fusion | flops 1611268096 | bytes 9969664 | tf_op jit(solution)/shard_map/transpose(jvp())/while/body/eval_jaxpr/hif,hfd->hid/dot_general | solution.py:119
  108.5 14.7 %all-gather.22.cloned.1.call-done = bf16[16,1024,64]{1,2,0:T(8,128)(2,1)} async-done(((bf16[8,1024,64]{1,2,0:T(8,128)(2,1)}), bf16[16,1024,64]{1,2,0:T(8,128)(2,1)}) %all-gather.22.cloned.1.call-update) | async-done | bytes 2097168 | tf_op jit(solution)/shard_map/all_gather | solution.py:62
  126.3 47.8 %all-gather.12.cloned.1.call-done = bf16[4,8,1024,64]{2,3,1,0:T(8,128)(2,1)} async-done(((bf16[1,8,1024,64]{2,3,1,0:T(8,128)(2,1)}), bf16[4,8,1024,64]{2,3,1,0:T(8,128)(2,1)}) %all-gather.12.cloned.1.call-update) | async-done | bytes 4194320 | tf_op jit(solution)/shard_map/all_gather | solution.py:41
  174.1 4.1 fusion.29
  184.9 39.4 %all-gather.16.cloned.1.call-done = bf16[4,8,1024,64]{2,3,1,0:T(8,128)(2,1)} async-done(((bf16[1,8,1024,64]{2,3,1,0:T(8,128)(2,1)}), bf16[4,8,1024,64]{2,3,1,0:T(8,128)(2,1)}) %all-gather.16.cloned.1.call-update) | async-done | bytes 4194320 | tf_op jit(solution)/shard_map/all_gather | solution.py:62
  224.3 4.1 fusion.28
  228.4 45.8 %all-gather.14.cloned.1.call-done = bf16[4,8,1024,64]{2,3,1,0:T(8,128)(2,1)} async-done(((bf16[1,8,1024,64]{2,3,1,0:T(8,128)(2,1)}), bf16[4,8,1024,64]{2,3,1,0:T(8,128)(2,1)}) %all-gather.14.cloned.1.call-update) | async-done | bytes 4194320 | tf_op jit(solution)/shard_map/all_gather | solution.py:41
  274.2 5.9 %fusion.8 = f32[8,1024,64]{1,2,0:T(8,128)S(1)} fusion(f32[8,1024,64]{1,2,0:T(8,128)} %param.15, bf16[4,8,1024,64]{2,3,1,0:T(8,128)(2,1)} %all-gather.14.cloned.1.call-done, pred[]{:T(512)S(6)} %gt.38, pred[]{:T(512)S(6)} %gt.39, pred[]{:T(512)S(6)} %gt.34, pred[]{:T(512)S(6)} %gt.30, pred[]{:T(512)S(6)} %gt.37, pred[]{:T(512)S(6)} %gt.36, pred[]{:T(512)S(6)} %gt.35, ...), kind=kLoop, calls=%fused_computation.32 | loop fusion | flops 15728640 | bytes 14680074 | tf_op jit(solution)/shard_map/add | solution.py:241
  280.1 8.8 %fusion.128 = f32[8,256,64]{1,2,0:T(8,128)S(1)} fusion(f32[8,256,1024]{1,2,0:T(8,128)} %bitcast.166, f32[8,1024,64]{1,2,0:T(8,128)S(1)} %fusion.8), kind=kOutput, calls=%fused_computation.197 | convolution fusion | flops 1610612736 | bytes 11010048 | tf_op jit(solution)/shard_map/jvp()/while/body/eval_jaxpr/hif,hfd->hid/dot_general | solution.py:119
  290.0 10.3 %fusion.119 = bf16[8,1,1024]{2,1,0:T(2,128)(2,1)S(1)} fusion(f32[8,256,1024]{1,2,0:T(8,128)} %bitcast.167, f32[8,256,1]{1,0,2:T(8,128)S(1)} %get-tuple-element.405), kind=kOutput, calls=%fused_computation.187 | convolution fusion | flops 25165824 | bytes 8413184 | tf_op jit(solution)/shard_map/transpose(jvp())/while/body/eval_jaxpr/hif,hf->hi/dot_general | solution.py:125
  302.1 9.0 %fusion.47 = f32[8,256,64]{1,2,0:T(8,128)} fusion(f32[8,256,1024]{1,2,0:T(8,128)} %bitcast.169), kind=kOutput, calls=%fused_computation.90 | convolution fusion | flops 1610612736 | bytes 8912896 | tf_op jit(solution)/shard_map/transpose(jvp())/while/body/eval_jaxpr/hjf,hjd->hfd/dot_general | solution.py:130
  311.7 9.2 %multiply_add_fusion = f32[8,256,1024]{2,1,0:T(8,128)} fusion(f32[8,1024]{1,0:T(8,128)S(1)} %fusion.68, f32[8,256]{1,0:T(8,128)S(1)} %get-tuple-element.406, f32[8,1024,64]{1,2,0:T(8,128)S(1)} %copy-done.5, f32[8,256]{1,0:T(8,128)S(1)} %get-tuple-element.403, f32[256,512]{0,1:T(8,128)S(1)} %copy.84), kind=kOutput, calls=%fused_computation.6 | convolution fusion | flops 1614938112 | bytes 11059200 | tf_op jit(solution)/shard_map/transpose(jvp())/while/body/eval_jaxpr/hif,hfd->hid/dot_general | solution.py:119
  320.9 9.1 %copy.91 = f32[8,256,1024]{1,2,0:T(8,128)} copy(f32[8,256,1024]{2,1,0:T(8,128)} %multiply_add_fusion) | data formatting | bytes 16777216 | tf_op jit(solution)/shard_map/transpose(jvp())/while/body/eval_jaxpr/hif,hfd->hid/add_any | solution.py:119
  332.4 9.4 %all_gather.69 = bf16[4,8,1024]{2,1,0:T(8,128)(2,1)S(1)} all-gather(bf16[1,8,1024]{2,1,0:T(8,128)(2,1)S(1)} %fusion.93), channel_id=1, replica_groups=mesh['seq_0'=4,'seq_1'=4,'seq_2'=2,'head'=4] {'seq_1'}, dimensions={0}, use_global_device_ids=true | all-gather | bytes 81920 | tf_op jit(solution)/shard_map/all_gather | solution.py:62
  341.8 10.8 %all_gather.70 = bf16[4,8,1024]{2,1,0:T(8,128)(2,1)S(1)} all-gather(bf16[1,8,1024]{2,1,0:T(8,128)(2,1)S(1)} %fusion.90), channel_id=1, replica_groups=mesh['seq_0'=4,'seq_1'=4,'seq_2'=2,'head'=4] {'seq_0'}, dimensions={0}, use_global_device_ids=true | all-gather | bytes 81920 | tf_op jit(solution)/shard_map/all_gather | solution.py:62
  353.5 6.2 %fusion.18 = f32[8,1024,64]{1,2,0:T(8,128)S(1)} fusion(f32[8,1024,64]{1,2,0:T(8,128)} %param.18, bf16[4,8,1024,64]{2,3,1,0:T(8,128)(2,1)} %all-gather.18.cloned.1.call-done, pred[]{:T(512)S(6)} %lt.44, pred[]{:T(512)S(6)} %lt.45, pred[]{:T(512)S(6)} %lt.40, pred[]{:T(512)S(6)} %lt.36, pred[]{:T(512)S(6)} %lt.43, pred[]{:T(512)S(6)} %lt.42, pred[]{:T(512)S(6)} %lt.41, ...), kind=kLoop, calls=%fused_computation.42 | loop fusion | flops 15728640 | bytes 14680074 | tf_op jit(solution)/shard_map/add | solution.py:255
  361.0 5.7 %broadcast_add_fusion = f32[8,256,1024]{2,1,0:T(8,128)} fusion(f32[8,1024]{1,0:T(8,128)S(1)} %fusion.81, bf16[8,256,64]{1,2,0:T(8,128)(2,1)S(1)} %bitcast.182, f32[8,1024,64]{1,2,0:T(8,128)S(1)} %fusion.18), kind=kOutput, calls=%fused_computation.7 | convolution fusion | flops 1612709888 | bytes 10780672 | tf_op jit(solution)/shard_map/transpose(jvp())/while/body/eval_jaxpr/hjf,hjd->hfd/dot_general | solution.py:170
  366.8 9.4 %copy.95 = f32[8,256,1024]{1,2,0:T(8,128)} copy(f32[8,256,1024]{2,1,0:T(8,128)} %broadcast_add_fusion) | data formatting | bytes 16777216 | tf_op jit(solution)/shard_map/transpose(jvp())/while/body/eval_jaxpr/hjf,hjd->hfd/add_any | solution.py:170
  379.2 8.9 %multiply_reduce_fusion.5 = (f32[8,256,32]{1,2,0:T(8,128)S(1)}, f32[8,256,32]{1,2,0:T(8,128)S(1)}) fusion(f32[8,256,32,32]{1,3,2,0:T(8,128)} %bitcast.174, f32[8,256,32]{1,2,0:T(8,128)S(1)} %get-tuple-element.407, f32[8,256,1024]{1,2,0:T(8,128)} %copy.91), kind=kLoop, calls=%fused_computation.5 | loop fusion | flops 8257536 | bytes 17563648 | tf_op jit(solution)/shard_map/transpose(jvp())/while/body/eval_jaxpr/reduce_sum | solution.py:103
  399.4 5.6 %fusion.130 = f32[8,256,64]{1,2,0:T(8,128)S(1)} fusion(f32[8,256,1024]{1,2,0:T(8,128)S(1)} %bitcast.172, f32[8,1024,64]{1,2,0:T(8,128)S(1)} %copy-done.7), kind=kOutput, calls=%fused_computation.199 | convolution fusion | flops 1610612736 | bytes 11010048 | tf_op jit(solution)/shard_map/transpose(jvp())/while/body/eval_jaxpr/hjf,hjd->hfd/dot_general | solution.py:170
  427.3 15.5 %all-gather.24.cloned.1.call-done = bf16[17039360]{0:T(1024)(128)(2,1)} async-done(((bf16[532480]{0:T(1024)(128)(2,1)}), bf16[17039360]{0:T(1024)(128)(2,1)}) %all-gather.24.cloned.1.call-update) | async-done | bytes 34078736 | tf_op jit(solution)/shard_map/all_gather | solution.py:92
  442.8 41.3 %reshape.429 = bf16[32,532480]{1,0:T(8,128)(2,1)} reshape(bf16[17039360]{0:T(1024)(128)(2,1)} %all-gather.24.cloned.1.call-done) | data formatting | bytes 68157440 | tf_op jit(solution)/shard_map/all_gather | solution.py:92
  484.1 22.7 %reduce_sum.170 = bf16[532480]{0:T(1024)(128)(2,1)S(1)} reduce(bf16[32,532480]{1,0:T(8,128)(2,1)} %reshape.429, bf16[]{:T(256)} %constant.166.clone.1), dimensions={0}, to_apply=%region_10.11 | reduce | flops 16506880 | bytes 35143680 | tf_op jit(solution)/shard_map/reduce_sum | solution.py:92
  508.2 4.3 reshape.415
  512.6 5.9 %add.293 = f32[8,1024,64]{2,1,0:T(8,128)} add(f32[8,1024,64]{2,1,0:T(8,128)} %copy.101, f32[8,1024,64]{2,1,0:T(8,128)} %reshape.415) | non-fusion elementwise | flops 524288 | bytes 6291456 | tf_op jit(solution)/shard_map/add | solution.py:272
  (150 shorter events, 92.9 us)
Async XLA Ops:
  7.2 21.5 %copy-start = (bf16[2048,512]{1,0:T(8,128)(2,1)S(1)}, bf16[2048,512]{1,0:T(8,128)(2,1)}, u32[]{:S(2)}) copy-start(bf16[2048,512]{1,0:T(8,128)(2,1)} %param.11) | copy-start | bytes 6291460
  7.2 7.1 %copy-start.27 = (bf16[256,512]{1,0:T(8,128)(2,1)S(1)}, bf16[256,512]{1,0:T(8,128)(2,1)}, u32[]{:S(2)}) copy-start(bf16[256,512]{1,0:T(8,128)(2,1)} %param.17) | copy-start | bytes 786436
  9.5 19.2 %all-to-all-start = ((bf16[4,256,512]{1,2,0:T(8,128)(2,1)}), bf16[4,256,512]{1,2,0:T(8,128)(2,1)}, u32[]{:S(2)}, u32[]{:S(2)}) async-start(bf16[4,256,512]{1,2,0:T(8,128)(2,1)} %broadcast_in_dim.136), calls=%async_computation | async-start | bytes 2097152 | tf_op jit(solution)/shard_map/all_to_all | solution.py:20
  14.3 91.2 %all-gather.20.cloned.1.call-start = ((), (), s32[]{:S(2)}) async-start(), calls=%async_computation.6 | async-start | bytes 3145728 | tf_op jit(solution)/shard_map/all_gather | solution.py:41
  28.7 2.1 copy-start.21
  85.9 37.3 %all-gather.22.cloned.1.call-start = ((), (), s32[]{:S(2)}) async-start(), calls=%async_computation.7 | async-start | bytes 3145728 | tf_op jit(solution)/shard_map/all_gather | solution.py:62
  91.3 4.4 copy-start.1
  105.4 68.7 %all-gather.12.cloned.1.call-start = ((), (), s32[]{:S(2)}) async-start(), calls=%async_computation.2 | async-start | bytes 5242880 | tf_op jit(solution)/shard_map/all_gather | solution.py:41
  108.5 115.8 %all-gather.16.cloned.1.call-start = ((), (), s32[]{:S(2)}) async-start(), calls=%async_computation.4 | async-start | bytes 5242880 | tf_op jit(solution)/shard_map/all_gather | solution.py:62
  126.2 148.0 %all-gather.14.cloned.1.call-start = ((), (), s32[]{:S(2)}) async-start(), calls=%async_computation.3 | async-start | bytes 5242880 | tf_op jit(solution)/shard_map/all_gather | solution.py:41
  178.2 175.3 %all-gather.18.cloned.1.call-start = ((), (), s32[]{:S(2)}) async-start(), calls=%async_computation.5 | async-start | bytes 5242880 | tf_op jit(solution)/shard_map/all_gather | solution.py:62
  228.4 214.5 %all-gather.24.cloned.1.call-start = ((), (), s32[]{:S(2)}) async-start(), calls=%async_computation.8 | async-start | bytes 35143680 | tf_op jit(solution)/shard_map/all_gather | solution.py:92
  280.1 8.8 %copy-start.4 = (f32[8,1024,64]{1,2,0:T(8,128)}, f32[8,1024,64]{1,2,0:T(8,128)S(1)}, u32[]{:S(2)}) copy-start(f32[8,1024,64]{1,2,0:T(8,128)S(1)} %fusion.8) | copy-start | bytes 6291460
  280.1 8.8 %copy-start.2 = (f32[8,256,256]{1,2,0:T(8,128)S(1)}, f32[8,256,256]{1,2,0:T(8,128)}, u32[]{:S(2)}) copy-start(f32[8,256,256]{1,2,0:T(8,128)} %get-tuple-element.412) | copy-start | bytes 6291460
  290.0 10.9 %copy-start.8 = (bf16[524288]{0:T(1024)(128)(2,1)S(1)}, bf16[524288]{0:T(1024)(128)(2,1)}, u32[]{:S(2)}) copy-start(bf16[524288]{0:T(1024)(128)(2,1)} %reshape.397) | copy-start | bytes 3145732
  302.1 9.0 %copy-start.25 = (bf16[8,1,1024]{2,1,0:T(2,128)(2,1)S(1)}, bf16[8,1,1024]{2,1,0:T(2,128)(2,1)}, u32[]{:S(2)}) copy-start(bf16[8,1,1024]{2,1,0:T(2,128)(2,1)} %copy-done.24) | copy-start | bytes 49156
  302.1 9.6 %copy-start.5 = (f32[8,1024,64]{1,2,0:T(8,128)S(1)}, f32[8,1024,64]{1,2,0:T(8,128)}, u32[]{:S(2)}) copy-start(f32[8,1024,64]{1,2,0:T(8,128)} %copy-done.4) | copy-start | bytes 6291460
  320.9 9.1 %copy-start.29 = (bf16[8,1,1024]{2,0,1:T(8,128)(2,1)S(1)}, bf16[8,1,1024]{2,0,1:T(8,128)(2,1)}, u32[]{:S(2)}) copy-start(bf16[8,1,1024]{2,0,1:T(8,128)(2,1)} %copy.135) | copy-start | bytes 49156
  376.2 17.4 %slice-start.2 = ((s8[8388608]{0:T(1024)(128)(4,1)}), s8[4194304]{0:T(1024)(128)(4,1)S(1)}, s32[]{:S(2)}) async-start(s8[8388608]{0:T(1024)(128)(4,1)} %bitcast.175), calls=%async_computation.11 | async-start | bytes 8388608
  379.2 14.3 %slice-start.3 = ((s8[8388608]{0:T(1024)(128)(4,1)}), s8[4194304]{0:T(1024)(128)(4,1)S(1)}, s32[]{:S(2)}) async-start(s8[8388608]{0:T(1024)(128)(4,1)} %bitcast.175), calls=%async_computation.12 | async-start | bytes 8388608
  388.1 2.1 copy-start.17
  389.5 2.7 copy-start.14
  389.6 3.3 copy-start.13
  390.2 9.0 %slice-start = ((s8[8388608]{0:T(1024)(128)(4,1)}), s8[4194304]{0:T(1024)(128)(4,1)S(1)}, s32[]{:S(2)}) async-start(s8[8388608]{0:T(1024)(128)(4,1)} %bitcast.170), calls=%async_computation.9 | async-start | bytes 8388608
  393.5 13.9 %copy-start.11 = (bf16[8,256,64]{1,2,0:T(8,128)(2,1)}, bf16[8,256,64]{1,2,0:T(8,128)(2,1)S(1)}, u32[]{:S(2)}) copy-start(bf16[8,256,64]{1,2,0:T(8,128)(2,1)S(1)} %fusion.40) | copy-start | bytes 786436
  393.6 4.2 copy-start.10
  393.6 5.6 %slice-start.1 = ((s8[8388608]{0:T(1024)(128)(4,1)}), s8[4194304]{0:T(1024)(128)(4,1)S(1)}, s32[]{:S(2)}) async-start(s8[8388608]{0:T(1024)(128)(4,1)} %bitcast.170), calls=%async_computation.10 | async-start | bytes 8388608
  399.4 5.6 %copy-start.3 = (f32[8,256,256]{1,2,0:T(8,128)S(1)}, f32[8,256,256]{1,2,0:T(8,128)}, u32[]{:S(2)}) copy-start(f32[8,256,256]{1,2,0:T(8,128)} %get-tuple-element.412) | copy-start | bytes 6291460
  399.4 5.7 %copy-start.23 = (f32[8,256,64]{1,2,0:T(8,128)S(1)}, f32[8,256,64]{1,2,0:T(8,128)}, u32[]{:S(2)}) copy-start(f32[8,256,64]{1,2,0:T(8,128)} %fusion.47) | copy-start | bytes 1572868
  407.4 2.6 copy-start.20
  412.6 13.8 %all-to-all-start.1 = ((bf16[4,256,512]{2,1,0:T(8,128)(2,1)}), bf16[4,256,512]{2,1,0:T(8,128)(2,1)S(1)}, u32[]{:S(2)}, u32[]{:S(2)}) async-start(bf16[4,256,512]{2,1,0:T(8,128)(2,1)} %bitcast.184), calls=%async_computation.1 | async-start | bytes 2097152 | tf_op jit(solution)/shard_map/all_to_all | solution.py:84
  518.5 3.8 copy-start.28
  (11 other events, 13.1 us)
Sparse Core Ops, SparseCore 0:
  86.1 17.6 all-gather.19
  105.5 17.6 all-gather.21
  124.9 49.1 all-gather.11
  175.6 48.5 all-gather.15
  225.8 48.3 all-gather.13
  275.7 48.5 all-gather.17
  326.6 116.2 all-gather.23
